TPU v7x, 512 devices: a whole 4x8x8 slice. The times are simulated.
512 devices in a mesh: task: 4 (over y_lo), tok: 128 (over z, y_hi, x, core).
Axes of the slice: x: 4, y: 8 (y_hi: 2, y_lo: 4; y = y_hi * 4 + y_lo), z: 8, core: 2. Of those that a mesh axis runs over, the one named last changes fastest.
Arguments:
- hidden: bfloat16 [4, 4096, 3584], P('task', 'tok'), may hold values from -6 to 6
- attn_out: bfloat16 [4, 4096, 3584], P('task', 'tok'), may hold values from -6 to 6
- gain_attn: bfloat16 [3584], replicated, may hold values from 0.5 to 1.5
- gain_mlp: bfloat16 [3584], replicated, may hold values from 0.5 to 1.5
- lengths: int32 [4, 2], P('task'), may hold values from 512 to 2048
Outputs:
- gram_attn: float32 [128, 112, 896], P('tok', 'task')
- gram_mlp: float32 [128, 112, 896], P('tok', 'task')
All inputs are finite; a program needn't handle non-finite values.
Results may differ from a plain program's by a relative error of at most 0.0044.
Values may be sent and summed in bfloat16 or wider, within the bound.
No kernel may reach another device: no remote copies, remote signals or barrier semaphores. Data moves between devices by JAX's collectives and lax.ppermute only.
A program may use at most 64 MiB of HBM per device.

v0:
```python
import jax
import jax.numpy as jnp
from jax import lax
from jax.sharding import Mesh
from jax.sharding import PartitionSpec as P

TOK = ("z", "yh", "x", "core")
YRING = ("yh", "task")


def normed(values, gain):
    scale = lax.rsqrt(jnp.mean(values * values, axis=-1, keepdims=True) + 1e-06)
    return values * scale * gain.astype(jnp.float32)


def per_device(hidden, attn_out, gain_attn, gain_mlp, lengths):
    rows = hidden.shape[1]
    width = hidden.shape[2]
    n_z, n_yh, n_x, n_core = (lax.axis_size(a) for a in TOK)
    n_task = lax.axis_size("task")
    tokens = rows * n_z * n_yh * n_x * n_core
    seq_len = tokens // lengths.shape[1]
    band = width // 4
    part = band // (n_x * n_core * n_task)
    z = lax.axis_index("z")
    core = lax.axis_index("core")
    place = lax.axis_index(TOK) * rows + jnp.arange(rows, dtype=jnp.int32)
    which = lax.axis_index(TOK) * rows // seq_len
    limit = lax.dynamic_index_in_dim(lengths[0], which, keepdims=False)
    live = (place - which * seq_len < limit).astype(jnp.float32)[:, None]
    first = hidden[0].astype(jnp.float32)
    x_attn = (normed(first, gain_attn) * live).astype(jnp.bfloat16)
    mixed = first + attn_out[0].astype(jnp.float32)
    x_mlp = (normed(mixed, gain_mlp) * live).astype(jnp.bfloat16)
    both = jnp.concatenate([x_attn, x_mlp], axis=1)
    seen = lax.all_gather(both, ("z", "core"), axis=0, tiled=True)

    def tile(at):
        left = lax.dynamic_slice_in_dim(seen, at * width + z // 2 * band, band, 1)
        right = lax.dynamic_slice_in_dim(seen, at * width + z % 2 * 2 * band, 2 * band, 1)
        full = lax.dot_general(
            left, right, (((0,), (0,)), ((), ())), preferred_element_type=jnp.float32
        )
        full = full.reshape(n_x, n_core, n_task, part, n_yh, band)
        return jnp.where(core == 0, full[:, 0], full[:, 1])

    parts = jnp.stack([tile(0), tile(1)])
    parts = parts.transpose(4, 2, 1, 0, 3, 5).astype(jnp.bfloat16)
    parts = parts.reshape(n_yh * n_task * n_x * 2 * part, band)
    ring = lax.psum_scatter(parts, YRING, scatter_dimension=0, tiled=True)
    ring = ring.reshape(n_x, 2 * part, band)
    ring = lax.all_to_all(ring, "x", split_axis=0, concat_axis=0, tiled=True)
    total = ring.astype(jnp.float32).sum(axis=0) * (1.0 / tokens)
    return (total[None, :part], total[None, part:])


def solution(mesh):
    n_task = mesh.shape["task"]
    grid = Mesh(mesh.devices.reshape(n_task, 8, 2, 4, 2), ("task",) + TOK)
    return jax.shard_map(
        per_device,
        mesh=grid,
        in_specs=(P("task", TOK, None), P("task", TOK, None), P(), P(), P("task", None)),
        out_specs=(P(TOK, "task", None), P(TOK, "task", None)),
        check_vma=False,
    )
```

profile of v0, /device:TPU:24, one launch (start us, length us, event | category | flops | bytes accessed | tf_op | source)
XLA Modules:
  0.0 179.4 jit_solution(12961962622690158551)
XLA Ops:
  7.2 0.0 copy-start
  7.2 0.0 all-gather.2.cloned.1.call-start
  7.3 0.7 convert_element_type.40
  8.0 0.7 convert_element_type.45
  8.7 0.0 copy-done
  8.7 0.6 constant_dynamic-slice_fusion
  9.2 0.6 compare_convert_fusion
  9.9 1.3 fusion.10
  11.2 1.3 fusion.13
  12.4 0.8 pad_maximum_fusion
  13.2 0.0 all-gather.2.cloned.1.call-update
  13.2 0.0 reduce-scatter.2.cloned.1.call-start
  13.3 58.8 %all-gather.2.cloned.1.call-done = bf16[512,7168]{1,0:T(8,128)(2,1)} async-done(((bf16[32,7168]{1,0:T(8,128)(2,1)}), bf16[512,7168]{1,0:T(8,128)(2,1)}) %all-gather.2.cloned.1.call-update) | async-done | bytes 7340048 | tf_op jit(solution)/shard_map/all_gather | solution.py:36
  72.1 5.4 %fusion.4 = bf16[896,1792]{1,0:T(8,128)(2,1)} fusion(bf16[512,7168]{1,0:T(8,128)(2,1)} %all-gather.2.cloned.1.call-done, s32[]{:T(128)S(6)} %select_n.75, s32[]{:T(128)S(6)} %select_n.74), kind=kOutput, calls=%fused_computation.7 | convolution fusion | flops 1644167168 | bytes 5963784 | tf_op jit(solution)/shard_map/dot_general | solution.py:41
  77.5 5.9 %reshape.88 = bf16[4,2,4,28,2,896]{5,4,3,2,1,0:T(2,128)(2,1)S(1)} reshape(bf16[896,1792]{1,0:T(8,128)(2,1)} %fusion.4) | data formatting | bytes 6422528 | tf_op jit(solution)/shard_map/reshape | solution.py:44
  83.5 5.4 %fusion.6 = bf16[896,1792]{1,0:T(8,128)(2,1)} fusion(bf16[512,7168]{1,0:T(8,128)(2,1)} %all-gather.2.cloned.1.call-done, s32[]{:T(128)S(6)} %select_n.71, s32[]{:T(128)S(6)} %select_n.69), kind=kOutput, calls=%fused_computation.9 | convolution fusion | flops 1644167168 | bytes 5963784 | tf_op jit(solution)/shard_map/dot_general | solution.py:41
  88.9 7.1 %reshape.87 = bf16[4,2,4,28,2,896]{5,4,3,2,1,0:T(2,128)(2,1)} reshape(bf16[896,1792]{1,0:T(8,128)(2,1)} %fusion.6) | data formatting | bytes 6422528 | tf_op jit(solution)/shard_map/reshape | solution.py:44
  96.0 4.1 %fusion.16 = (bf16[4,1,4,28,2,896]{5,4,3,2,1,0:T(2,128)(2,1)S(1)}, bf16[4,1,4,28,2,896]{5,4,3,2,1,0:T(2,128)(2,1)S(1)}) fusion(bf16[4,2,4,28,2,896]{5,4,3,2,1,0:T(2,128)(2,1)} %reshape.87), kind=kLoop, calls=%fused_computation.31 | loop fusion | bytes 6422528 | tf_op jit(solution)/shard_map/slice | solution.py:45
  100.1 2.2 %fusion.17 = (bf16[4,1,4,28,2,896]{5,4,3,2,1,0:T(2,128)(2,1)S(1)}, bf16[4,1,4,28,2,896]{5,4,3,2,1,0:T(2,128)(2,1)S(1)}) fusion(bf16[4,2,4,28,2,896]{5,4,3,2,1,0:T(2,128)(2,1)S(1)} %reshape.88), kind=kLoop, calls=%fused_computation.32 | loop fusion | bytes 6422528 | tf_op jit(solution)/shard_map/slice | solution.py:45
  102.3 0.5 fusion.2
  102.8 0.5 fusion.3
  103.3 2.3 %maximum_bitcast_fusion = bf16[2,4,4,2,28,896]{5,4,3,2,1,0:T(8,128)(2,1)} fusion(bf16[1,4,4,28,2,896]{5,3,0,1,2,4:T(8,128)(2,1)S(1)} %fusion.3, bf16[1,4,4,28,2,896]{5,3,0,1,2,4:T(8,128)(2,1)S(1)} %fusion.2), kind=kLoop, calls=%fused_computation | loop fusion | flops 1605632 | bytes 6422528 | tf_op jit(solution)/shard_map/convert_element_type | solution.py:48
  105.6 6.0 %reshape.89 = bf16[1792,896]{1,0:T(8,128)(2,1)} reshape(bf16[2,4,4,2,28,896]{5,4,3,2,1,0:T(8,128)(2,1)} %maximum_bitcast_fusion) | data formatting | bytes 6422528 | tf_op jit(solution)/shard_map/reshape | solution.py:49
  111.6 0.0 reduce-scatter.2.cloned.1.call-update
  111.6 47.7 %reduce-scatter.2.cloned.1.call-done = bf16[224,896]{1,0:T(8,128)(2,1)} async-done(((bf16[1792,896]{1,0:T(8,128)(2,1)}), bf16[224,896]{1,0:T(8,128)(2,1)}) %reduce-scatter.2.cloned.1.call-update) | async-done | bytes 401424 | tf_op jit(solution)/shard_map/reduce_scatter | solution.py:50
  159.3 11.7 %all_to_all.5 = bf16[4,56,896]{2,1,0:T(8,128)(2,1)S(1)} all-to-all(bf16[4,56,896]{2,1,0:T(8,128)(2,1)} %bitcast.20), channel_id=1, replica_groups=mesh['task'=4,'z'=8,'yh'=2,'x'=4,'core'=2] {'x'}, dimensions={0} | all-to-all | bytes 802816 | tf_op jit(solution)/shard_map/all_to_all | solution.py:52
  171.0 0.1 convert_reduce_fusion
  171.1 0.7 broadcast_in_dim.5
  171.8 0.7 broadcast_in_dim.4
  (3 shorter events, 0.0 us)
Async XLA Ops:
  7.2 1.5 copy-start
  7.2 64.9 %all-gather.2.cloned.1.call-start = ((), (), s32[]{:S(2)}) async-start(), calls=%async_computation.2 | async-start | bytes 7798784 | tf_op jit(solution)/shard_map/all_gather | solution.py:36
  13.2 146.0 %reduce-scatter.2.cloned.1.call-start = ((), (), s32[]{:S(2)}) async-start(), calls=%async_computation.3 | async-start | bytes 3612672 | tf_op jit(solution)/shard_map/reduce_scatter | solution.py:50
Sparse Core Ops, SparseCore 0:
  13.4 58.7 all-gather.1
  111.7 47.4 reduce-scatter.1
where the time goes:
time: 180 us; the launch traced here: 179 us
  waiting for transfers between devices  106 us (59%)
  local copies, waits for them, and re-layouts  27.3 us (15%)
  between operations  14.2 us (8%)
  blocking collectives  11.7 us (6%)
  matrix products  10.8 us (6%)
  other arithmetic  8.75 us (5%)
    all_gather x1, waiting for transfers between devices, per_device(): seen = lax.all_gather(both, ('z', 'core'), axis=0, tiled=True)  58.8 us
    reduce_scatter x1, waiting for transfers between devices, per_device(): ring = lax.psum_scatter(parts, YRING, scatter_dimension=0, tiled=True)  47.7 us
    reshape x2, local copies, waits for them, and re-layouts, tile(): full = full.reshape(n_x, n_core, n_task, part, n_yh, band)  13 us
    all_to_all x1, blocking collectives, per_device(): ring = lax.all_to_all(ring, 'x', split_axis=0, concat_axis=0, tiled=True)  11.7 us
    dot_general x2, matrix products, tile(): lax.dot_general(left, right, (((0,), (0,)), ((), ())), preferred_element_...  10.8 us
    slice x2, local copies, waits for them, and re-layouts, tile(): return jnp.where(core == 0, full[:, 0], full[:, 1])  6.31 us
    reshape x1, local copies, waits for them, and re-layouts, per_device(): parts = parts.reshape(n_yh * n_task * n_x * 2 * part, band)  6 us
  transfers between devices with their start and end apart: 2, of which 2 were waited for; matrix products, arithmetic and copies ran while one was open for 0% of the time, Pallas kernels for 0%

commit v1 on v0

--- a/solution.py
+++ b/solution.py
@@ -33,7 +33,10 @@
     mixed = first + attn_out[0].astype(jnp.float32)
     x_mlp = (normed(mixed, gain_mlp) * live).astype(jnp.bfloat16)
     both = jnp.concatenate([x_attn, x_mlp], axis=1)
-    seen = lax.all_gather(both, ("z", "core"), axis=0, tiled=True)
+    devices = lax.axis_size(("z", "core"))
+    blocks = jnp.stack([both for _ in range(devices)])
+    blocks = lax.all_to_all(blocks, ("z", "core"), split_axis=0, concat_axis=0)
+    seen = jnp.concatenate(blocks, axis=0)
 
     def tile(at):
         left = lax.dynamic_slice_in_dim(seen, at * width + z // 2 * band, band, 1)

time: 180 us -> 296 us (1.64)
  waiting for transfers between devices: 106 us -> 210 us
  starting transfers between devices: 0.08 us -> 10.5 us
    all_to_all x0 -> x1, waiting for transfers between devices: none -> 162 us  [per_device(): blocks = lax.all_to_all(blocks, ('z', 'core'), split_axis=0, concat_axis=0)]
    all_gather x1 -> x0, waiting for transfers between devices: 58.8 us -> none  [per_device(): seen = lax.all_gather(both, ('z', 'core'), axis=0, tiled=True)]
    all_to_all x0 -> x1, starting transfers between devices: none -> 10.5 us  [per_device(): blocks = lax.all_to_all(blocks, ('z', 'core'), split_axis=0, concat_axis=0)]
    another operation x0 -> x1, local copies, waits for them, and re-layouts: none -> 3.9 us  [per_device(): blocks = jnp.stack([both for _ in range(devices)])]
where the time goes in v1:
time: 296 us; the launch traced here: 295 us
  waiting for transfers between devices  210 us (71%)
  local copies, waits for them, and re-layouts  29.9 us (10%)
  between operations  14.2 us (5%)
  blocking collectives  11.5 us (4%)
  matrix products  10.8 us (4%)
  starting transfers between devices  10.5 us (4%)
  other arithmetic  7.99 us (3%)
    all_to_all x1, waiting for transfers between devices, per_device(): blocks = lax.all_to_all(blocks, ('z', 'core'), split_axis=0, concat_axis=0)  162 us
    reduce_scatter x1, waiting for transfers between devices, per_device(): ring = lax.psum_scatter(parts, YRING, scatter_dimension=0, tiled=True)  48.5 us
    reshape x2, local copies, waits for them, and re-layouts, tile(): full = full.reshape(n_x, n_core, n_task, part, n_yh, band)  11.8 us
    all_to_all x1, blocking collectives, per_device(): ring = lax.all_to_all(ring, 'x', split_axis=0, concat_axis=0, tiled=True)  11.5 us
    dot_general x2, matrix products, tile(): lax.dot_general(left, right, (((0,), (0,)), ((), ())), preferred_element_...  10.8 us
    all_to_all x1, starting transfers between devices, per_device(): blocks = lax.all_to_all(blocks, ('z', 'core'), split_axis=0, concat_axis=0)  10.5 us
    slice x2, local copies, waits for them, and re-layouts, tile(): return jnp.where(core == 0, full[:, 0], full[:, 1])  6.18 us
    reshape x1, local copies, waits for them, and re-layouts, per_device(): parts = parts.reshape(n_yh * n_task * n_x * 2 * part, band)  6.02 us
  transfers between devices with their start and end apart: 2, of which 2 were waited for; matrix products, arithmetic and copies ran while one was open for 0% of the time, Pallas kernels for 0%

profile of v1, /device:TPU:24, one launch (start us, length us, event | category | flops | bytes accessed | tf_op | source)
XLA Modules:
  0.0 295.1 jit_solution(10196504562488684678)
XLA Ops:
  7.2 0.0 copy-start
  7.2 0.7 convert_element_type.40
  7.9 0.7 convert_element_type.45
  8.6 0.0 copy-done
  8.6 0.6 constant_dynamic-slice_fusion
  9.2 0.6 compare_convert_fusion
  9.8 1.3 fusion.10
  11.1 1.3 fusion.13
  12.4 3.9 %stack.5 = bf16[16,32,7168]{2,1,0:T(8,128)(2,1)} broadcast(bf16[32,7168]{1,0:T(8,128)(2,1)S(1)} %pad_maximum_fusion), dimensions={1,2} | broadcast | bytes 7798784 | tf_op jit(solution)/shard_map/stack | solution.py:37
  16.3 10.5 %all-to-all-start = ((bf16[16,32,7168]{2,1,0:T(8,128)(2,1)}), bf16[16,32,7168]{2,1,0:T(8,128)(2,1)}, u32[]{:S(2)}, u32[]{:S(2)}) async-start(bf16[16,32,7168]{2,1,0:T(8,128)(2,1)} %stack.5), calls=%async_computation | async-start | bytes 14680064 | tf_op jit(solution)/shard_map/all_to_all | solution.py:38
  26.8 0.0 reduce-scatter.2.cloned.1.call-start
  26.9 161.7 %all-to-all-done = bf16[16,32,7168]{2,1,0:T(8,128)(2,1)} async-done(((bf16[16,32,7168]{2,1,0:T(8,128)(2,1)}), bf16[16,32,7168]{2,1,0:T(8,128)(2,1)}, u32[]{:S(2)}, u32[]{:S(2)}) %all-to-all-start) | async-done | bytes 7340064 | tf_op jit(solution)/shard_map/all_to_all | solution.py:38
  188.5 5.4 %fusion.6 = bf16[896,1792]{1,0:T(8,128)(2,1)} fusion(bf16[512,7168]{1,0:T(8,128)(2,1)} %bitcast.4, s32[]{:T(128)S(6)} %select_n.71, s32[]{:T(128)S(6)} %select_n.69), kind=kOutput, calls=%fused_computation.9 | convolution fusion | flops 1644167168 | bytes 5963784 | tf_op jit(solution)/shard_map/dot_general | solution.py:44
  193.9 5.9 %reshape.93 = bf16[4,2,4,28,2,896]{5,4,3,2,1,0:T(2,128)(2,1)S(1)} reshape(bf16[896,1792]{1,0:T(8,128)(2,1)} %fusion.6) | data formatting | bytes 6422528 | tf_op jit(solution)/shard_map/reshape | solution.py:47
  199.8 4.0 %fusion.16 = (bf16[4,1,4,28,2,896]{5,4,3,2,1,0:T(2,128)(2,1)}, bf16[4,1,4,28,2,896]{5,4,3,2,1,0:T(2,128)(2,1)}) fusion(bf16[4,2,4,28,2,896]{5,4,3,2,1,0:T(2,128)(2,1)S(1)} %reshape.93), kind=kLoop, calls=%fused_computation.31 | loop fusion | bytes 6422528 | tf_op jit(solution)/shard_map/slice | solution.py:48
  203.8 5.4 %fusion.4 = bf16[896,1792]{1,0:T(8,128)(2,1)} fusion(bf16[512,7168]{1,0:T(8,128)(2,1)} %bitcast.4, s32[]{:T(128)S(6)} %select_n.75, s32[]{:T(128)S(6)} %select_n.74), kind=kOutput, calls=%fused_computation.7 | convolution fusion | flops 1644167168 | bytes 5963784 | tf_op jit(solution)/shard_map/dot_general | solution.py:44
  209.2 5.9 %reshape.94 = bf16[4,2,4,28,2,896]{5,4,3,2,1,0:T(2,128)(2,1)S(1)} reshape(bf16[896,1792]{1,0:T(8,128)(2,1)} %fusion.4) | data formatting | bytes 6422528 | tf_op jit(solution)/shard_map/reshape | solution.py:47
  215.1 0.0 copy-start.1
  215.1 0.0 copy-start.2
  215.1 2.2 fusion.17
  217.4 0.0 copy-done.1
  217.4 0.0 copy-done.2
  217.4 0.5 fusion.2
  217.9 0.5 fusion.3
  218.4 2.3 maximum_bitcast_fusion
  220.7 6.0 %reshape.95 = bf16[1792,896]{1,0:T(8,128)(2,1)} reshape(bf16[2,4,4,2,28,896]{5,4,3,2,1,0:T(8,128)(2,1)} %maximum_bitcast_fusion) | data formatting | bytes 6422528 | tf_op jit(solution)/shard_map/reshape | solution.py:52
  226.7 0.0 reduce-scatter.2.cloned.1.call-update
  226.7 48.5 %reduce-scatter.2.cloned.1.call-done = bf16[224,896]{1,0:T(8,128)(2,1)} async-done(((bf16[1792,896]{1,0:T(8,128)(2,1)}), bf16[224,896]{1,0:T(8,128)(2,1)}) %reduce-scatter.2.cloned.1.call-update) | async-done | bytes 401424 | tf_op jit(solution)/shard_map/reduce_scatter | solution.py:53
  275.2 11.5 %all_to_all.10 = bf16[4,56,896]{2,1,0:T(8,128)(2,1)S(1)} all-to-all(bf16[4,56,896]{2,1,0:T(8,128)(2,1)} %bitcast.21), channel_id=1, replica_groups=mesh['task'=4,'z'=8,'yh'=2,'x'=4,'core'=2] {'x'}, dimensions={0} | all-to-all | bytes 802816 | tf_op jit(solution)/shard_map/all_to_all | solution.py:55
  286.7 0.1 convert_reduce_fusion
  286.8 0.7 broadcast_in_dim.4
  287.5 0.7 broadcast_in_dim.5
  (4 shorter events, 0.1 us)
Async XLA Ops:
  7.2 1.4 copy-start
  16.3 172.2 %all-to-all-start = ((bf16[16,32,7168]{2,1,0:T(8,128)(2,1)}), bf16[16,32,7168]{2,1,0:T(8,128)(2,1)}, u32[]{:S(2)}, u32[]{:S(2)}) async-start(bf16[16,32,7168]{2,1,0:T(8,128)(2,1)} %stack.5), calls=%async_computation | async-start | bytes 14680064 | tf_op jit(solution)/shard_map/all_to_all | solution.py:38
  26.8 248.4 %reduce-scatter.2.cloned.1.call-start = ((), (), s32[]{:S(2)}) async-start(), calls=%async_computation.3 | async-start | bytes 3612672 | tf_op jit(solution)/shard_map/reduce_scatter | solution.py:53
  215.1 2.2 copy-start.1
  215.1 2.2 copy-start.2
Sparse Core Ops, SparseCore 0:
  226.9 48.3 reduce-scatter.1
